TPU v7x, 128 devices: a whole 4x4x4 slice. The times are simulated.
128 devices in a mesh: dp: 16 (over y, z), tensor: 8 (over x, core).
Axes of the slice: x: 4, y: 4, z: 4, core: 2. Of those that a mesh axis runs over, the one named last changes fastest.
Arguments:
- hidden: bfloat16 [8192, 5120], P('dp'), may hold values from -48 to 48
- head_weight: bfloat16 [5120, 8192], P(None, 'tensor'), may hold values from -0.069877124 to 0.069877124
- token_ids: int32 [8192], P('dp'), may hold values from 0 to 8191
- old_logprob: float32 [8192], P('dp'), may hold values from -12.5 to 0.3
- rewards: int32 [128], P('dp'), may hold values from 0 to 1, as said below
- lengths: int32 [128], P('dp'), may hold values from 1 to 64, as said below
- group_ids: int32 [128], P('dp'), may hold values from 0 to 7, as said below
- loss_scale: float32 [], replicated, may hold values from 8192 to 32768
Outputs:
- loss: float32 [], replicated
- grad_hidden: float32 [8192, 5120], P('dp', 'tensor')
- grad_weight: float32 [5120, 8192], P('dp', 'tensor')
Inputs may be any that keep to these rules, and one draw needn't show every extreme that they name: `group_ids`: each group number names exactly 16 rollouts. `rewards`: some group holds both a 0 and a 1. `lengths`: some index of dp holds only rollouts of length 64 whose prompts hold both a 0 and a 1.
All inputs are finite; a program needn't handle non-finite values.
Results may differ from a plain program's by a relative error of at most 0.003.
Values may be sent and summed in bfloat16 or wider, within the bound.
A program may use at most 192 MiB of HBM per device.

v0:
```python
import jax
import jax.numpy as jnp
from jax import lax
from jax.sharding import PartitionSpec as P

GROUP = 16


clip_low = 0.2
clip_high = 0.28


def sent_to_all(array, axis):
    length = lax.axis_size(axis)
    return lax.all_to_all(
        jnp.broadcast_to(array[None], (length, *array.shape)), axis, 0, 0, tiled=True
    )


def over_copies(array, axis):
    return sent_to_all(array, axis).sum(axis=0)


def in_one(arrays, axis):
    vector, at, done = (jnp.concatenate([a.reshape(-1) for a in arrays]), 0, [])
    subtotal = over_copies(vector, axis)
    for a in arrays:
        done.append(subtotal[at : at + a.size].reshape(a.shape))
        at += a.size
    return tuple(done)


def contract_rows(first_operand, second_operand):
    return lax.dot_general(
        first_operand, second_operand, (((0,), (0,)), ((), ())), preferred_element_type=jnp.float32
    )


def contract_cols(first_operand, second_operand):
    return lax.dot_general(
        first_operand, second_operand, (((1,), (1,)), ((), ())), preferred_element_type=jnp.float32
    )


def run_blocks(block_fn, initial):
    return block_fn(0, initial)


def group_terms(member, group_wins, reward_float):
    group_alive = jnp.logical_and(group_wins > 0.5, group_wins < GROUP - 0.5).astype(jnp.float32)
    center = group_wins / GROUP
    spread = jnp.where(group_alive > 0.5, jnp.sqrt(group_wins * (GROUP - group_wins)) / GROUP, 1.0)
    roll_alive = jnp.sum(member * group_alive[None, :], axis=1)
    roll_center = jnp.sum(member * center[None, :], axis=1)
    roll_spread = jnp.sum(member * spread[None, :], axis=1)
    advantage = roll_alive * (reward_float - roll_center) / roll_spread
    return (group_alive, roll_alive, advantage)


def policy_terms(log_prob, old_rows, adv_rows, weight_rows, factor):
    prob_ratio = jnp.exp(log_prob - old_rows)
    clipped = jnp.clip(prob_ratio, 1.0 - clip_low, 1.0 + clip_high)
    token_loss = -jnp.minimum(prob_ratio * adv_rows, clipped * adv_rows)
    active = prob_ratio * adv_rows <= clipped * adv_rows
    coefficient = jnp.where(active, -adv_rows * prob_ratio, 0.0) * weight_rows * factor
    return (token_loss, coefficient)


def shards(hidden, head_weight, token_ids, old_logprob, rewards, lengths, group_ids, loss_scale):
    row_count, model_width = hidden.shape
    roll_count = rewards.shape[0]
    response = row_count // roll_count
    vocab_part = head_weight.shape[1]
    data_size = lax.axis_size("dp")
    group_count = roll_count * data_size // GROUP
    member = (group_ids[:, None] == jnp.arange(group_count, dtype=jnp.int32)[None, :]).astype(
        jnp.float32
    )
    reward_float = rewards.astype(jnp.float32)
    length_float = lengths.astype(jnp.float32)
    local_wins = jnp.sum(member * reward_float[:, None], axis=0)
    local_tokens = jnp.sum(member * length_float[:, None], axis=0)
    group_wins, group_tokens = in_one((local_wins, local_tokens), "dp")
    group_alive, roll_alive, advantage = group_terms(member, group_wins, reward_float)
    token_count = jnp.sum(group_alive * group_tokens)
    divisor = jnp.maximum(token_count, 1.0)
    factor = loss_scale / divisor
    position = jnp.arange(response, dtype=jnp.int32)
    inside = (position[None, :] < lengths[:, None]).astype(jnp.float32)
    token_weight = (roll_alive[:, None] * inside).reshape(row_count)
    token_adv = jnp.broadcast_to(advantage[:, None], (roll_count, response)).reshape(row_count)

    def logit_block(block_index, current):
        block_logits = jnp.dot(hidden, head_weight, preferred_element_type=jnp.float32)
        return block_logits

    logits = run_blocks(logit_block, jnp.zeros((row_count, vocab_part), jnp.float32))
    row_top = lax.pmax(jnp.max(logits, axis=1), "tensor")
    shifted = jnp.exp(logits - row_top[:, None])
    column = (
        jnp.arange(vocab_part, dtype=jnp.int32)[None, :] + lax.axis_index("tensor") * vocab_part
    )
    is_target = column == token_ids[:, None]
    row_total, target = lax.psum(
        (jnp.sum(shifted, axis=1), jnp.sum(jnp.where(is_target, logits, 0.0), axis=1)), "tensor"
    )
    softmax_rows = shifted / row_total[:, None]
    log_prob = target - row_top - jnp.log(row_total)
    token_loss, coefficient = policy_terms(log_prob, old_logprob, token_adv, token_weight, factor)
    logit_grad = (coefficient[:, None] * (is_target.astype(jnp.float32) - softmax_rows)).astype(
        jnp.bfloat16
    )

    def grad_block(block_index, current):
        return contract_cols(logit_grad, head_weight)

    grad_part = run_blocks(grad_block, jnp.zeros((row_count, model_width), jnp.float32))
    columns = lax.all_to_all(hidden, "dp", split_axis=1, concat_axis=0, tiled=True)
    grad_weight = contract_rows(columns, lax.all_gather(logit_grad, "dp", axis=0, tiled=True))
    grad_cols = lax.psum_scatter(grad_part, "tensor", scatter_dimension=1, tiled=True)
    loss_total = over_copies(jnp.sum(token_weight * token_loss), "dp")
    return (loss_total / divisor, grad_cols, grad_weight)


def solution(mesh):
    return jax.shard_map(
        shards,
        mesh=mesh,
        in_specs=(
            P("dp", None),
            P(None, "tensor"),
            P("dp"),
            P("dp"),
            P("dp"),
            P("dp"),
            P("dp"),
            P(),
        ),
        out_specs=(P(), P("dp", "tensor"), P("dp", "tensor")),
        check_vma=False,
    )
```

profile of v0, /device:TPU:0, one launch (start us, length us, event | category | flops | bytes accessed | tf_op | source)
XLA Modules:
  0.0 243.2 jit_solution(2442096091829942554)
XLA Ops:
  8.0 0.7 convert_element_type.17
  8.7 0.7 convert_element_type.18
  9.3 0.7 select_reduce_fusion.4
  10.1 0.1 pad_maximum_fusion
  10.1 0.6 broadcast_in_dim.14
  10.7 8.2 %all-to-all-start = ((f32[16,1,16]{2,1,0:T(1,128)}), f32[16,1,16]{2,1,0:T(1,128)S(1)}, u32[]{:S(2)}, u32[]{:S(2)}) async-start(f32[16,1,16]{2,1,0:T(1,128)} %broadcast_in_dim.14), calls=%async_computation | async-start | bytes 16384 | tf_op jit(solution)/shard_map/all_to_all | solution.py:15
  18.9 0.0 all-gather.2.cloned.1.call-start
  19.0 0.0 copy-start
  19.0 10.0 %fusion.9 = (f32[512]{0:T(512)S(1)}, f32[512,1024]{1,0:T(8,128)S(1)}) fusion(bf16[512,5120]{1,0:T(8,128)(2,1)} %param.8, bf16[5120,1024]{1,0:T(8,128)(2,1)} %param.9), kind=kOutput, calls=%fused_computation.32 | convolution fusion | flops 5369232896 | bytes 17827840 | tf_op jit(solution)/shard_map/dot_general | solution.py:94
  29.0 0.0 copy-start.2
  29.0 0.0 copy-start.3
  29.1 0.0 copy-start.4
  29.1 0.0 copy-start.1
  29.1 14.3 %pmax.7 = f32[512]{0:T(512)S(1)} all-reduce(f32[512]{0:T(512)S(1)} %get-tuple-element.17), channel_id=1, replica_groups=mesh['dp'=16,'tensor'=8] {'tensor'}, use_global_device_ids=true, to_apply=%region_7.8 | all-reduce | flops 512 | bytes 4096 | tf_op jit(solution)/shard_map/pmax | solution.py:98
  43.4 0.0 copy-done
  43.4 0.7 fusion
  44.1 12.4 %all-reduce = (f32[512]{0:T(512)S(1)}, f32[512]{0:T(512)S(1)}) all-reduce(f32[512]{0:T(512)S(1)} %get-tuple-element.4, f32[512]{0:T(512)S(1)} %get-tuple-element.3), channel_id=1, replica_groups=mesh['dp'=16,'tensor'=8] {'tensor'}, use_global_device_ids=true, to_apply=%region_9.10 | all-reduce | flops 1024 | bytes 8192 | tf_op jit(solution)/shard_map/psum | solution.py:104
  57.2 0.0 all-to-all-done
  57.2 0.7 select_reduce_fusion.5
  57.9 0.0 copy-done.2
  57.9 0.2 select_reduce_fusion.1
  58.1 0.0 copy-done.3
  58.1 0.1 fusion.5
  58.2 0.1 mul.101
  58.2 0.0 copy-done.4
  58.2 0.1 broadcast_in_dim.17
  58.3 0.1 reshape.46
  59.1 0.0 copy-done.1
  59.1 1.6 fusion.3
  60.8 0.0 all-gather.2.cloned.1.call-update
  60.8 0.0 reduce-scatter.2.cloned.1.call-start
  60.8 11.0 %fusion.10 = f32[512,5120]{1,0:T(8,128)} fusion(bf16[512,1024]{1,0:T(8,128)(2,1)} %fusion.3, bf16[5120,1024]{1,0:T(8,128)(2,1)} %param.9), kind=kOutput, calls=%fused_computation.33 | convolution fusion | flops 5368709120 | bytes 22020096 | tf_op jit(solution)/shard_map/dot_general | solution.py:40
  71.9 0.0 reduce-scatter.2.cloned.1.call-update
  71.9 0.6 multiply_reduce_fusion
  72.5 1.2 broadcast_in_dim.18
  73.8 6.9 %all-to-all-start.1 = ((f32[16,1,1]{2,1,0:T(1,128)}), f32[16,1,1]{2,1,0:T(1,128)S(1)}, u32[]{:S(2)}, u32[]{:S(2)}) async-start(f32[16,1,1]{2,1,0:T(1,128)} %broadcast_in_dim.18), calls=%async_computation.1 | async-start | bytes 16384 | tf_op jit(solution)/shard_map/all_to_all | solution.py:15
  80.7 8.0 %copy.17 = bf16[512,5120]{0,1:T(8,128)(2,1)} copy(bf16[512,5120]{1,0:T(8,128)(2,1)} %param.8) | data formatting | bytes 10485760 | tf_op args[0]
  88.8 0.0 all-to-all-done.1
  88.8 7.3 %all-to-all-start.2 = ((bf16[512,16,320]{0,2,1:T(8,128)(2,1)}), bf16[512,16,320]{0,2,1:T(8,128)(2,1)}, u32[]{:S(2)}, u32[]{:S(2)}) async-start(bf16[512,16,320]{0,2,1:T(8,128)(2,1)} %bitcast.13), calls=%async_computation.3 | async-start | bytes 10485760 | tf_op jit(solution)/shard_map/all_to_all | solution.py:118
  96.0 0.6 reduce_sum.108
  97.3 108.8 %all-to-all-done.2 = bf16[512,16,320]{0,2,1:T(8,128)(2,1)} async-done(((bf16[512,16,320]{0,2,1:T(8,128)(2,1)}), bf16[512,16,320]{0,2,1:T(8,128)(2,1)}, u32[]{:S(2)}, u32[]{:S(2)}) %all-to-all-start.2) | async-done | bytes 5242912 | tf_op jit(solution)/shard_map/all_to_all | solution.py:118
  206.1 5.6 %copy.20 = bf16[16,40,8,512]{3,2,0,1:T(8,128)(2,1)} copy(bf16[16,40,8,512]{3,2,1,0:T(8,128)(2,1)} %bitcast.4) | data formatting | bytes 10485760 | tf_op jit(solution)/shard_map/all_to_all | solution.py:118
  211.7 11.3 %all-gather.2.cloned.1.call-done = bf16[8192,1024]{1,0:T(8,128)(2,1)} async-done(((bf16[512,1024]{1,0:T(8,128)(2,1)}), bf16[8192,1024]{1,0:T(8,128)(2,1)}) %all-gather.2.cloned.1.call-update) | async-done | bytes 16777232 | tf_op jit(solution)/shard_map/all_gather | solution.py:119
  223.0 11.6 %convolution_bitcast_fusion = f32[320,1024]{1,0:T(8,128)} fusion(bf16[8192,320]{0,1:T(8,128)(2,1)} %bitcast.14, bf16[8192,1024]{1,0:T(8,128)(2,1)} %all-gather.2.cloned.1.call-done), kind=kOutput, calls=%fused_computation.8 | convolution fusion | flops 5368709120 | bytes 23330816 | tf_op jit(solution)/shard_map/dot_general | solution.py:34
  234.6 0.0 reduce-scatter.2.cloned.1.call-done
  (5 shorter events, 0.1 us)
Async XLA Ops:
  10.7 46.4 %all-to-all-start = ((f32[16,1,16]{2,1,0:T(1,128)}), f32[16,1,16]{2,1,0:T(1,128)S(1)}, u32[]{:S(2)}, u32[]{:S(2)}) async-start(f32[16,1,16]{2,1,0:T(1,128)} %broadcast_in_dim.14), calls=%async_computation | async-start | bytes 16384 | tf_op jit(solution)/shard_map/all_to_all | solution.py:15
  18.9 204.1 %all-gather.2.cloned.1.call-start = ((), (), s32[]{:S(2)}) async-start(), calls=%async_computation.5 | async-start | bytes 17825792 | tf_op jit(solution)/shard_map/all_gather | solution.py:119
  19.0 24.4 %copy-start = (s32[512]{0:T(512)S(1)}, s32[512]{0:T(512)}, u32[]{:S(2)}) copy-start(s32[512]{0:T(512)} %param.10) | copy-start | bytes 6148
  29.0 28.8 %copy-start.2 = (s32[8]{0:T(128)S(1)}, s32[8]{0:T(128)}, u32[]{:S(2)}) copy-start(s32[8]{0:T(128)} %param.14) | copy-start | bytes 100
  29.0 29.0 %copy-start.3 = (s32[8]{0:T(128)S(1)}, s32[8]{0:T(128)}, u32[]{:S(2)}) copy-start(s32[8]{0:T(128)} %param.13) | copy-start | bytes 100
  29.1 29.2 %copy-start.4 = (s32[8]{0:T(128)S(1)}, s32[8]{0:T(128)}, u32[]{:S(2)}) copy-start(s32[8]{0:T(128)} %param.12) | copy-start | bytes 100
  29.1 30.0 %copy-start.1 = (f32[512]{0:T(512)S(1)}, f32[512]{0:T(512)}, u32[]{:S(2)}) copy-start(f32[512]{0:T(512)} %param.11) | copy-start | bytes 6148
  60.8 173.8 %reduce-scatter.2.cloned.1.call-start = ((), (), s32[]{:S(2)}) async-start(), calls=%async_computation.4 | async-start | bytes 11796480 | tf_op jit(solution)/shard_map/reduce_scatter | solution.py:120
  73.8 15.0 %all-to-all-start.1 = ((f32[16,1,1]{2,1,0:T(1,128)}), f32[16,1,1]{2,1,0:T(1,128)S(1)}, u32[]{:S(2)}, u32[]{:S(2)}) async-start(f32[16,1,1]{2,1,0:T(1,128)} %broadcast_in_dim.18), calls=%async_computation.1 | async-start | bytes 16384 | tf_op jit(solution)/shard_map/all_to_all | solution.py:15
  88.8 117.4 %all-to-all-start.2 = ((bf16[512,16,320]{0,2,1:T(8,128)(2,1)}), bf16[512,16,320]{0,2,1:T(8,128)(2,1)}, u32[]{:S(2)}, u32[]{:S(2)}) async-start(bf16[512,16,320]{0,2,1:T(8,128)(2,1)} %bitcast.13), calls=%async_computation.3 | async-start | bytes 10485760 | tf_op jit(solution)/shard_map/all_to_all | solution.py:118
Sparse Core Ops, SparseCore 0:
  60.9 162.0 all-gather.1
Sparse Core Ops, SparseCore 1:
  72.0 61.1 reduce-scatter.1
where the time goes:
time: 245 us; the launch traced here: 243 us
  waiting for transfers between devices  120 us (49%)
  matrix products  32.6 us (13%)
  blocking collectives  26.7 us (11%)
  starting transfers between devices  22.5 us (9%)
  between operations  18.7 us (8%)
  local copies, waits for them, and re-layouts  15.8 us (6%)
  other arithmetic  6.68 us (3%)
    all_to_all x1, waiting for transfers between devices, shards(): lax.all_to_all(hidden, 'dp', split_axis=1, concat_axis=0, tiled=True)  109 us
    all_to_all x2, starting transfers between devices, sent_to_all(): lax.all_to_all(jnp.broadcast_to(array[None], (length, *array.shape)), axi...  15.1 us
    pmax x1, blocking collectives, shards(): row_top = lax.pmax(jnp.max(logits, axis=1), 'tensor')  14.3 us
    psum x1, blocking collectives, shards(): lax.psum((jnp.sum(shifted, axis=1), jnp.sum(jnp.where(is_target, logits,...  12.4 us
    dot_general x1, matrix products, contract_rows(): lax.dot_general(first_operand, second_operand, (((0,), (0,)), ((), ())),...  11.6 us
    all_gather x1, waiting for transfers between devices, shards(): lax.all_gather(logit_grad, 'dp', axis=0, tiled=True)  11.3 us
    dot_general x1, matrix products, contract_cols(): lax.dot_general(first_operand, second_operand, (((1,), (1,)), ((), ())),...  11 us
    dot_general x1, matrix products, logit_block(): jnp.dot(hidden, head_weight, preferred_element_type=jnp.float32)  10 us
  transfers between devices with their start and end apart: 5, of which 2 were waited for; matrix products, arithmetic and copies ran while one was open for 20% of the time, Pallas kernels for 0%

commit v1 on v0

v1 whole, which is shorter than its diff:
```python
import functools

import jax
import jax.numpy as jnp
from jax import lax
from jax.experimental import pallas as pl
from jax.experimental.pallas import tpu as pltpu
from jax.sharding import PartitionSpec as P

GROUP = 16
CLIP_LOW = 0.2
CLIP_HIGH = 0.28
RING = 4
CORES = 2
LANES = 128
MESH = pl.DeviceIdType.MESH
F32 = jnp.float32
BF16 = jnp.bfloat16


class Sems:
    sizes = dict(
        group_y=RING,
        group_z=RING,
        loss_y=RING,
        loss_z=RING,
        stats=RING * CORES,
        hid_y=RING,
        hid_x=RING * 2,
        hid_relay=RING,
        hid_core=RING,
        w_core=RING,
        lg_core=RING,
        lg_own=RING * 2,
        lg_relay=RING * 2,
        x_half=2,
        x_side=2,
        z_half=RING * 2,
        z_side=RING * 2,
    )

    def __init__(self, send, recv):
        self.send, self.recv, self.base, at = send, recv, {}, 0
        for name, size in self.sizes.items():
            self.base[name] = at
            at += size

    @classmethod
    def total(cls):
        return sum(cls.sizes.values())

    def of(self, name, index):
        at = self.base[name] + index
        return self.send.at[at], self.recv.at[at]


def contract_last(a, b):
    return lax.dot_general(a, b, (((1,), (1,)), ((), ())), preferred_element_type=F32)


def kernel(
    h_hbm, w_hbm, tok_ref, old_ref, rew_ref, len_ref, gid_ref, scale_ref,
    loss_ref, gh_ref, gw_ref,
    hv, wv, hq, wp, prob, lgg, lgp, ht, asend, tok_col, coef_col, mul_col, stat_col,
    stat_send, stat_recv, group_y, group_z, loss_y, loss_z,
    x_acc, x_opp, x_side, x_half_in, x_side_in,
    z_acc, z_opp, z_side, z_half_in, z_side_in,
    load_sem, send_sem, recv_sem,
):
    tokens, width = hv.shape
    vocab = wv.shape[1]
    chunk = vocab // RING
    half_cols = width // RING // CORES
    z_rows = width // (RING * RING)
    dp, tensor = lax.axis_index("dp"), lax.axis_index("tensor")
    y, z = dp // RING, dp % RING
    x, core = tensor // CORES, tensor % CORES
    sems = Sems(send_sem, recv_sem)
    started = []

    def at_y(k):
        return ((y + k) % RING * RING + z, tensor)

    def at_z(k):
        return (y * RING + (z + k) % RING, tensor)

    def at_x(k):
        return (dp, (x + k) % RING * CORES + core)

    def at_tensor(k):
        return (dp, (tensor + k) % (RING * CORES))

    partner = (dp, x * CORES + 1 - core)

    def remote(src, dst, name, index, device):
        send, recv = sems.of(name, index)
        return pltpu.make_async_remote_copy(
            src_ref=src, dst_ref=dst, send_sem=send, recv_sem=recv, device_id=device, device_id_type=MESH
        )

    def put(src, dst, name, index, device):
        copy = remote(src, dst, name, index, device)
        copy.start()
        started.append(copy)

    def arrived(dst, name, index):
        remote(dst, dst, name, index, partner).wait_recv()

    k_size = 1024
    k_count = width // k_size
    quarter = [
        pltpu.make_async_copy(
            h_hbm.at[
                pl.ds(pl.multiple_of(x * LANES, LANES), LANES),
                pl.ds(pl.multiple_of(q * half_cols * CORES + core * half_cols, LANES), half_cols),
            ],
            hq.at[q],
            load_sem.at[q],
        )
        for q in range(RING)
    ]
    for copy in quarter:
        copy.start()

    def load_pair(k):
        return (
            pltpu.make_async_copy(
                h_hbm.at[:, pl.ds(pl.multiple_of(k * k_size, k_size), k_size)],
                hv.at[:, pl.ds(pl.multiple_of(k * k_size, k_size), k_size)],
                load_sem.at[RING + 2 * k],
            ),
            pltpu.make_async_copy(
                w_hbm.at[pl.ds(pl.multiple_of(k * k_size, k_size), k_size), :],
                wv.at[pl.ds(pl.multiple_of(k * k_size, k_size), k_size), :],
                load_sem.at[RING + 2 * k + 1],
            ),
        )

    for k in range(k_count):
        for copy in load_pair(k):
            copy.start()

    barrier = pltpu.get_barrier_semaphore()
    peers = (
        [at_y(k) for k in range(1, RING)]
        + [at_z(k) for k in range(1, RING)]
        + [at_tensor(k) for k in range(1, RING * CORES)]
    )
    for device in peers:
        pl.semaphore_signal(barrier, inc=1, device_id=device, device_id_type=MESH)
    pl.semaphore_wait(barrier, len(peers))

    rolls = rew_ref.shape[0]
    roll_tokens = tokens // rolls
    lane8 = lax.broadcasted_iota(jnp.int32, (8, LANES), 1)
    row8 = lax.broadcasted_iota(jnp.int32, (8, LANES), 0)
    local = jnp.zeros((8, LANES), F32)
    for i in range(rolls):
        value = jnp.where(row8 == 0, rew_ref[i].astype(F32), len_ref[i].astype(F32))
        local += jnp.where((lane8 == gid_ref[i]) & (row8 < 2), value, 0.0)
    group_y[y] = local

    half = pl.ds(pl.multiple_of(core * half_cols, 16), half_cols)
    for q in range(RING):
        quarter[q].wait()
        for b in range(half_cols // LANES):
            asend[q, b * LANES : (b + 1) * LANES, :] = hq[q, :, b * LANES : (b + 1) * LANES].T
    ht[y, x, half, :] = asend[y]
    for k in range(1, RING):
        put(group_y.at[y], group_y.at[y], "group_y", k, at_y(k))
    for k in (2, 1, 3):
        put(asend.at[(y + k) % RING], ht.at[y, x, half, :], "hid_y", k, at_y(k))

    def share_over_x(j):
        block = ht.at[(y + j) % RING, x, half, :]
        put(block, block, "hid_x", 2 * j, at_x(3))
        put(block, block, "hid_x", 2 * j + 1, at_x(1))

    def relay_over_x(j):
        source = (y + j) % RING
        right_block = ht.at[source, (x + 1) % RING, half, :]
        left_block = ht.at[source, (x + 3) % RING, half, :]
        arrived(right_block, "hid_x", 2 * j)
        arrived(left_block, "hid_x", 2 * j + 1)
        if j < 2:
            put(left_block, left_block, "hid_relay", j, at_x(1))
        else:
            put(right_block, right_block, "hid_relay", j, at_x(3))

    def hand_to_partner(j):
        source = (y + j) % RING
        arrived(ht.at[source, (x + 2) % RING, half, :], "hid_relay", j)
        block = ht.at[source, :, half, :]
        put(block, block, "hid_core", j, partner)

    share_over_x(0)

    tok = tok_ref[...].astype(F32)
    for r in range(tokens // LANES):
        tok_col[r * LANES : (r + 1) * LANES, :] = jnp.broadcast_to(tok[r : r + 1, :], (LANES, LANES)).T

    for k in range(k_count):
        for copy in load_pair(k):
            copy.wait()

        @pl.loop(0, vocab // 256)
        def _(n, k=k):
            cols = pl.ds(pl.multiple_of(n * 256, 256), 256)
            term = jnp.dot(
                hv[:, k * k_size : (k + 1) * k_size],
                wv[k * k_size : (k + 1) * k_size, cols],
                preferred_element_type=F32,
            )
            if k == 0:
                prob[:, cols] = term
            else:
                prob[:, cols] += term

    for q in range(RING):
        rows = pl.ds(pl.multiple_of((q * CORES + 1 - core) * half_cols, 16), half_cols)
        put(wv.at[rows, :], wp.at[q], "w_core", q, partner)

    step = 32
    lane_step = lax.broadcasted_iota(jnp.int32, (step, LANES), 1)
    column = lax.broadcasted_iota(jnp.int32, (step, vocab), 1).astype(F32)
    first_col = (tensor * vocab).astype(F32)

    @pl.loop(0, tokens // step)
    def _(i):
        rows = pl.ds(pl.multiple_of(i * step, step), step)
        block = prob[rows, :]
        top = jnp.max(block, axis=1, keepdims=True)
        shifted = jnp.exp(block - top)
        prob[rows, :] = shifted
        total = jnp.sum(shifted, axis=1, keepdims=True)
        wanted = jnp.tile(tok_col[rows, :], (1, vocab // LANES)) - first_col
        picked = jnp.sum(jnp.where(column == wanted, block, 0.0), axis=1, keepdims=True)
        stat_col[rows, :] = jnp.where(lane_step == 0, top, jnp.where(lane_step == 1, total, picked))

    for r in range(tokens // LANES):
        flipped = stat_col[r * LANES : (r + 1) * LANES, :].T
        for s in range(3):
            stat_send[s * 4 + r : s * 4 + r + 1, :] = flipped[s : s + 1, :]
    stat_send[12:16, :] = jnp.zeros((4, LANES), F32)
    stat_recv[tensor] = stat_send[...]
    for k in range(1, RING * CORES):
        put(stat_send, stat_recv.at[tensor], "stats", k, at_tensor(k))

    for k in range(1, RING):
        arrived(group_y.at[(y + RING - k) % RING], "group_y", k)
    group_z[z] = group_y[0] + group_y[1] + group_y[2] + group_y[3]
    for k in range(1, RING):
        put(group_z.at[z], group_z.at[z], "group_z", k, at_z(k))

    for k in (1, 3, 2):
        arrived(ht.at[(y + RING - k) % RING, x, half, :], "hid_y", k)
        share_over_x(RING - k)

    for k in range(1, RING * CORES):
        arrived(stat_recv.at[(tensor + RING * CORES - k) % (RING * CORES)], "stats", k)
    row_top = stat_recv[0, 0:4, :]
    for q in range(1, RING * CORES):
        row_top = jnp.maximum(row_top, stat_recv[q, 0:4, :])
    row_total = jnp.zeros_like(row_top)
    target = jnp.zeros_like(row_top)
    for q in range(RING * CORES):
        row_total += stat_recv[q, 4:8, :] * jnp.exp(stat_recv[q, 0:4, :] - row_top)
        target += stat_recv[q, 8:12, :]
    own_scale = jnp.exp(stat_send[0:4, :] - row_top)

    for k in range(1, RING):
        arrived(group_z.at[(z + RING - k) % RING], "group_z", k)
    groups = group_z[0] + group_z[1] + group_z[2] + group_z[3]
    group_wins, group_tokens = groups[0:1, :], groups[1:2, :]
    group_alive = ((group_wins > 0.5) & (group_wins < GROUP - 0.5)).astype(F32)
    token_count = jnp.sum(group_alive * group_tokens, axis=1, keepdims=True)
    divisor = jnp.maximum(token_count, 1.0)
    factor = scale_ref[0] / divisor

    lane4 = lax.broadcasted_iota(jnp.int32, (4, LANES), 1)
    row4 = lax.broadcasted_iota(jnp.int32, (4, LANES), 0)
    token_index = row4 * LANES + lane4
    lane1 = lax.broadcasted_iota(jnp.int32, (1, LANES), 1)
    wins = jnp.zeros((4, LANES), F32)
    reward = jnp.zeros((4, LANES), F32)
    length = jnp.zeros((4, LANES), jnp.int32)
    for i in range(rolls):
        mine = (token_index // roll_tokens) == i
        roll_wins = jnp.sum(jnp.where(lane1 == gid_ref[i], group_wins, 0.0), axis=1, keepdims=True)
        wins = jnp.where(mine, roll_wins, wins)
        reward = jnp.where(mine, rew_ref[i].astype(F32), reward)
        length = jnp.where(mine, len_ref[i], length)
    alive = ((wins > 0.5) & (wins < GROUP - 0.5)).astype(F32)
    spread = jnp.where(alive > 0.5, jnp.sqrt(wins * (GROUP - wins)) / GROUP, 1.0)
    token_adv = alive * (reward - wins / GROUP) / spread
    token_weight = jnp.where(token_index % roll_tokens < length, alive, 0.0)

    log_prob = target - row_top - jnp.log(row_total)
    ratio = jnp.exp(log_prob - old_ref[...])
    clipped = jnp.clip(ratio, 1.0 - CLIP_LOW, 1.0 + CLIP_HIGH)
    token_loss = -jnp.minimum(ratio * token_adv, clipped * token_adv)
    active = ratio * token_adv <= clipped * token_adv
    coefficient = jnp.where(active, -token_adv * ratio, 0.0) * token_weight * factor
    multiplier = coefficient * own_scale / row_total
    weighted = jnp.sum(token_weight * token_loss, axis=1, keepdims=True)
    local_loss = weighted[0:1] + weighted[1:2] + weighted[2:3] + weighted[3:4]

    for r in range(tokens // LANES):
        rows = slice(r * LANES, (r + 1) * LANES)
        coef_col[rows, :] = jnp.broadcast_to(coefficient[r : r + 1, :], (LANES, LANES)).T
        mul_col[rows, :] = jnp.broadcast_to(multiplier[r : r + 1, :], (LANES, LANES)).T

    column_chunk = lax.broadcasted_iota(jnp.int32, (64, chunk), 1).astype(F32)

    def send_chunk(n):
        block = lgg.at[y, n]
        put(block, block, "lg_own", 2 * n, at_y(3))
        put(block, block, "lg_own", 2 * n + 1, at_y(1))

    def relay_chunk(n):
        from_right, from_left = lgg.at[(y + 1) % RING, n], lgg.at[(y + 3) % RING, n]
        low, high = pl.ds(0, tokens // 2), pl.ds(tokens // 2, tokens // 2)
        arrived(from_right, "lg_own", 2 * n)
        arrived(from_left, "lg_own", 2 * n + 1)
        put(from_left.at[low], from_left.at[low], "lg_relay", 2 * n, at_y(1))
        put(from_right.at[high], from_right.at[high], "lg_relay", 2 * n + 1, at_y(3))

    for n in range(RING):

        @pl.loop(0, tokens // 64)
        def _(i, n=n):
            rows = pl.ds(pl.multiple_of(i * 64, 64), 64)
            wanted = jnp.tile(tok_col[rows, :], (1, chunk // LANES)) - (first_col + n * chunk)
            coef = jnp.tile(coef_col[rows, :], (1, chunk // LANES))
            mul = jnp.tile(mul_col[rows, :], (1, chunk // LANES))
            grad = jnp.where(column_chunk == wanted, coef, 0.0) - prob[rows, n * chunk : (n + 1) * chunk] * mul
            lgg[y, n, rows, :] = grad.astype(BF16)

        if n < 2:
            send_chunk(n)
        put(lgg.at[y, n], lgp.at[n], "lg_core", n, partner)

    loss_y[y] = jnp.broadcast_to(local_loss, (8, LANES))
    for k in range(1, RING):
        put(loss_y.at[y], loss_y.at[y], "loss_y", k, at_y(k))

    for n in range(RING):
        arrived(lgp.at[n], "lg_core", n)
        arrived(wp.at[n], "w_core", n)

    def hidden_block(offset):
        q = (x + offset) % RING
        rows = pl.ds(pl.multiple_of((q * CORES + core) * half_cols, 16), half_cols)
        result = None
        for n in range(RING):
            cols = slice(n * chunk, (n + 1) * chunk)
            term = contract_last(lgg[y, n], wv[rows, cols]) + contract_last(lgp[n], wp[q, :, cols])
            result = term if result is None else result + term
        return result

    x_opp[...] = hidden_block(2).astype(BF16)
    mid = tokens // 2
    put(x_opp.at[pl.ds(0, mid)], x_half_in.at[0], "x_half", 0, at_x(3))
    put(x_opp.at[pl.ds(mid, mid)], x_half_in.at[1], "x_half", 1, at_x(1))
    for j in (0, 3, 1, 2):
        relay_over_x(j)

    @pl.loop(0, 3)
    def _(j):
        x_acc[j] = hidden_block(j + 3)

    relay_chunk(0)
    send_chunk(2)
    for j in (0, 3, 1, 2):
        hand_to_partner(j)

    arrived(x_half_in.at[0], "x_half", 0)
    x_side[0, 0:mid, :] = (x_acc[0, 0:mid, :] + x_half_in[0].astype(F32)).astype(BF16)
    x_side[0, mid:, :] = x_acc[0, mid:, :].astype(BF16)
    put(x_side.at[0], x_side_in.at[0], "x_side", 0, at_x(3))
    arrived(x_half_in.at[1], "x_half", 1)
    x_side[1, 0:mid, :] = x_acc[2, 0:mid, :].astype(BF16)
    x_side[1, mid:, :] = (x_acc[2, mid:, :] + x_half_in[1].astype(F32)).astype(BF16)
    put(x_side.at[1], x_side_in.at[1], "x_side", 1, at_x(1))

    relay_chunk(1)
    send_chunk(3)
    for j in range(RING):
        other = pl.ds(pl.multiple_of((1 - core) * half_cols, 16), half_cols)
        arrived(ht.at[(y + j) % RING, :, other, :], "hid_core", j)

    low_rows = z_rows // 2

    def weight_block(n, offset):
        rows = pl.ds(pl.multiple_of((z + offset) % RING * z_rows, 16), z_rows)
        result = None
        for s in range(RING):
            for b in range(RING // 2):
                left = jnp.concatenate([ht[s, 2 * b, rows, :], ht[s, 2 * b + 1, rows, :]], axis=1)
                term = jnp.dot(left, lgg[s, n, b * 256 : (b + 1) * 256, :], preferred_element_type=F32)
                result = term if result is None else result + term
        return result

    def weight_chunk(n):
        low, high = pl.ds(0, tokens // 2), pl.ds(tokens // 2, tokens // 2)
        arrived(lgg.at[(y + 2) % RING, n, low], "lg_relay", 2 * n)
        arrived(lgg.at[(y + 2) % RING, n, high], "lg_relay", 2 * n + 1)
        z_opp[n] = weight_block(n, 2).astype(BF16)
        put(z_opp.at[n, pl.ds(0, low_rows)], z_half_in.at[n, 0], "z_half", 2 * n, at_z(3))
        put(z_opp.at[n, pl.ds(low_rows, low_rows)], z_half_in.at[n, 1], "z_half", 2 * n + 1, at_z(1))

        @pl.loop(0, 3)
        def _(j):
            z_acc[n, j] = weight_block(n, j + 3)

    def pass_sides(n):
        arrived(z_half_in.at[n, 0], "z_half", 2 * n)
        z_side[n, 0, 0:low_rows, :] = (z_acc[n, 0, 0:low_rows, :] + z_half_in[n, 0].astype(F32)).astype(BF16)
        z_side[n, 0, low_rows:, :] = z_acc[n, 0, low_rows:, :].astype(BF16)
        put(z_side.at[n, 0], z_side_in.at[n, 0], "z_side", 2 * n, at_z(3))
        arrived(z_half_in.at[n, 1], "z_half", 2 * n + 1)
        z_side[n, 1, 0:low_rows, :] = z_acc[n, 2, 0:low_rows, :].astype(BF16)
        z_side[n, 1, low_rows:, :] = (z_acc[n, 2, low_rows:, :] + z_half_in[n, 1].astype(F32)).astype(BF16)
        put(z_side.at[n, 1], z_side_in.at[n, 1], "z_side", 2 * n + 1, at_z(1))

    def finish_chunk(n):
        arrived(z_side_in.at[n, 0], "z_side", 2 * n)
        arrived(z_side_in.at[n, 1], "z_side", 2 * n + 1)
        gw_ref[:, n * chunk : (n + 1) * chunk] = (
            z_acc[n, 1] + z_side_in[n, 0].astype(F32) + z_side_in[n, 1].astype(F32)
        )

    weight_chunk(0)
    for k in range(1, RING):
        arrived(loss_y.at[(y + RING - k) % RING], "loss_y", k)
    loss_z[z] = loss_y[0] + loss_y[1] + loss_y[2] + loss_y[3]
    for k in range(1, RING):
        put(loss_z.at[z], loss_z.at[z], "loss_z", k, at_z(k))
    relay_chunk(2)
    weight_chunk(1)
    pass_sides(0)
    relay_chunk(3)
    pass_sides(1)

    arrived(x_side_in.at[0], "x_side", 0)
    arrived(x_side_in.at[1], "x_side", 1)
    gh_ref[...] = x_acc[1] + x_side_in[0].astype(F32) + x_side_in[1].astype(F32)

    weight_chunk(2)
    for k in range(1, RING):
        arrived(loss_z.at[(z + RING - k) % RING], "loss_z", k)
    loss_total = loss_z[0] + loss_z[1] + loss_z[2] + loss_z[3]
    loss_ref[...] = loss_total[0:1, 0:1] / divisor
    finish_chunk(0)
    pass_sides(2)
    finish_chunk(1)
    weight_chunk(3)
    finish_chunk(2)
    pass_sides(3)
    finish_chunk(3)
    for copy in started:
        copy.wait_send()


def shards(hidden, head_weight, token_ids, old_logprob, rewards, lengths, group_ids, loss_scale):
    tokens, width = hidden.shape
    vocab = head_weight.shape[1]
    chunk = vocab // RING
    half_cols = width // RING // CORES
    z_rows = width // (RING * RING)
    rows = tokens // LANES
    hbm = pl.BlockSpec(memory_space=pl.ANY)
    vmem = pl.BlockSpec(memory_space=pltpu.VMEM)
    smem = pl.BlockSpec(memory_space=pltpu.SMEM)
    loss, grad_hidden, grad_weight = pl.pallas_call(
        kernel,
        out_shape=(
            jax.ShapeDtypeStruct((1, 1), F32),
            jax.ShapeDtypeStruct((tokens, half_cols), F32),
            jax.ShapeDtypeStruct((z_rows, vocab), F32),
        ),
        in_specs=[hbm, hbm, vmem, vmem, smem, smem, smem, smem],
        out_specs=(vmem, vmem, vmem),
        scratch_shapes=[
            pltpu.VMEM((tokens, width), BF16),
            pltpu.VMEM((width, vocab), BF16),
            pltpu.VMEM((RING, LANES, half_cols), BF16),
            pltpu.VMEM((RING, half_cols, vocab), BF16),
            pltpu.VMEM((tokens, vocab), F32),
            pltpu.VMEM((RING, RING, tokens, chunk), BF16),
            pltpu.VMEM((RING, tokens, chunk), BF16),
            pltpu.VMEM((RING, RING, half_cols * CORES, LANES), BF16),
            pltpu.VMEM((RING, half_cols, LANES), BF16),
            pltpu.VMEM((tokens, LANES), F32),
            pltpu.VMEM((tokens, LANES), F32),
            pltpu.VMEM((tokens, LANES), F32),
            pltpu.VMEM((tokens, LANES), F32),
            pltpu.VMEM((16, LANES), F32),
            pltpu.VMEM((RING * CORES, 16, LANES), F32),
            pltpu.VMEM((RING, 8, LANES), F32),
            pltpu.VMEM((RING, 8, LANES), F32),
            pltpu.VMEM((RING, 8, LANES), F32),
            pltpu.VMEM((RING, 8, LANES), F32),
            pltpu.VMEM((3, tokens, half_cols), F32),
            pltpu.VMEM((tokens, half_cols), BF16),
            pltpu.VMEM((2, tokens, half_cols), BF16),
            pltpu.VMEM((2, tokens // 2, half_cols), BF16),
            pltpu.VMEM((2, tokens, half_cols), BF16),
            pltpu.VMEM((RING, 3, z_rows, chunk), F32),
            pltpu.VMEM((RING, z_rows, chunk), BF16),
            pltpu.VMEM((RING, 2, z_rows, chunk), BF16),
            pltpu.VMEM((RING, 2, z_rows // 2, chunk), BF16),
            pltpu.VMEM((RING, 2, z_rows, chunk), BF16),
            pltpu.SemaphoreType.DMA((RING + 2 * (width // 1024),)),
            pltpu.SemaphoreType.DMA((Sems.total(),)),
            pltpu.SemaphoreType.DMA((Sems.total(),)),
        ],
        compiler_params=pltpu.CompilerParams(
            collective_id=0, has_side_effects=True, vmem_limit_bytes=66_000_000
        ),
        name="policy_step",
    )(
        hidden,
        head_weight,
        token_ids.reshape(rows, LANES),
        old_logprob.reshape(rows, LANES),
        rewards,
        lengths,
        group_ids,
        loss_scale.reshape(1),
    )
    return (loss.reshape(()), grad_hidden, grad_weight)


def solution(mesh):
    return jax.shard_map(
        shards,
        mesh=mesh,
        in_specs=(
            P("dp", None),
            P(None, "tensor"),
            P("dp"),
            P("dp"),
            P("dp"),
            P("dp"),
            P("dp"),
            P(),
        ),
        out_specs=(P(), P("dp", "tensor"), P("dp", "tensor")),
        check_vma=False,
    )
```

time: 245 us -> 89.6 us (0.37)
  waiting for transfers between devices: 120 us -> 0 us
  Pallas kernels: 0 us -> 82.8 us
  matrix products: 32.6 us -> 0 us
  blocking collectives: 26.7 us -> 0 us
  starting transfers between devices: 22.5 us -> 0 us
  between operations: 18.7 us -> 2.98 us
  local copies, waits for them, and re-layouts: 15.8 us -> 3.62 us
  other arithmetic: 6.68 us -> 0 us
    all_to_all x3 -> x0, waiting for transfers between devices: 109 us -> none  [the longest x1 109 us: shards(): lax.all_to_all(hidden, 'dp', split_axis=1, concat_axis=0, tiled=True)]
    pallas_call x0 -> x1, Pallas kernels: none -> 82.8 us  [shards(): pl.pallas_call(kernel, out_shape=(jax.ShapeDtypeStruct((1, 1), F32), jax....]
    dot_general x3 -> x0, matrix products: 32.6 us -> none  [the longest x1 11.6 us: contract_rows(): lax.dot_general(first_operand, second_operand, (((0,), (0,)), ((), ())),...]
    all_to_all x3 -> x0, starting transfers between devices: 22.4 us -> none  [the longest x2 15.1 us: sent_to_all(): lax.all_to_all(jnp.broadcast_to(array[None], (length, *array.shape)), axi...]
    pmax x1 -> x0, blocking collectives: 14.3 us -> none  [shards(): row_top = lax.pmax(jnp.max(logits, axis=1), 'tensor')]
    psum x1 -> x0, blocking collectives: 12.4 us -> none  [shards(): lax.psum((jnp.sum(shifted, axis=1), jnp.sum(jnp.where(is_target, logits,...]
    all_gather x1 -> x0, waiting for transfers between devices: 11.3 us -> none  [shards(): lax.all_gather(logit_grad, 'dp', axis=0, tiled=True)]
    all_to_all x1 -> x0, local copies, waits for them, and re-layouts: 5.6 us -> none  [shards(): lax.all_to_all(hidden, 'dp', split_axis=1, concat_axis=0, tiled=True)]
  transfers between devices with their start and end apart: 5 -> 0, of which waited for: 2 -> 0; matrix products, arithmetic and copies ran while one was open for 20% -> 0% of each run, Pallas kernels for 0% -> 0%
where the time goes in v1:
time: 89.6 us; the launch traced here: 89.4 us
  Pallas kernels  82.8 us (92%)
  local copies, waits for them, and re-layouts  3.62 us (4%)
  between operations  2.98 us (3%)
    pallas_call x1, Pallas kernels, shards(): pl.pallas_call(kernel, out_shape=(jax.ShapeDtypeStruct((1, 1), F32), jax....  82.8 us
    unnamed x4, local copies, waits for them, and re-layouts  3.62 us

profile of v1, /device:TPU:0, one launch (start us, length us, event | category | flops | bytes accessed | tf_op | source)
XLA Modules:
  0.0 89.4 jit_solution(4483178154820169753)
XLA Ops:
  1.3 82.8 %policy_step.1 = (f32[1,1]{1,0:T(1,128)}, f32[512,640]{1,0:T(8,128)}, f32[320,1024]{1,0:T(8,128)}) custom-call(bf16[512,5120]{1,0:T(8,128)(2,1)} %h_hbm.1, bf16[5120,1024]{1,0:T(8,128)(2,1)} %w_hbm.1, s32[4,128]{1,0:T(4,128)} %bitcast.5, f32[4,128]{1,0:T(4,128)} %bitcast.6, s32[8]{0:T(128)} %rew_ref.1, s32[8]{0:T(128)} %len_ref.1, s32[8]{0:T(128)} %gid_ref.1, ...), custom_call_target="tpu_custom_call" | custom-call | tf_op jit(solution)/shard_map/policy_step/pallas_call | solution.py:475
  84.6 0.0 copy-start
  84.6 2.6 %copy.16 = f32[512,640]{1,0:T(8,128)} copy(f32[512,640]{1,0:T(8,128)} %get-tuple-element.13) | data formatting | bytes 2621440
  87.2 0.0 copy-done
  87.2 1.1 %copy.17 = f32[320,1024]{1,0:T(8,128)} copy(f32[320,1024]{1,0:T(8,128)S(1)} %copy-done) | data formatting | bytes 2621440
Async XLA Ops:
  84.6 2.6 %copy-start = (f32[320,1024]{1,0:T(8,128)S(1)}, f32[320,1024]{1,0:T(8,128)}, u32[]{:S(2)}) copy-start(f32[320,1024]{1,0:T(8,128)} %get-tuple-element.14) | copy-start | bytes 3932164

commit v2 on v1

v2 whole, which is shorter than its diff:
```python
import math

import jax
import jax.numpy as jnp
from jax import lax
from jax.experimental import pallas as pl
from jax.experimental.pallas import tpu as pltpu
from jax.sharding import PartitionSpec as P

GROUP = 16
CLIP_LOW = 0.2
CLIP_HIGH = 0.28
RING = 4
CORES = 2
LANES = 128
MESH = pl.DeviceIdType.MESH
PIECES = ((0, 2), (2, 2), (4, 2), (6, 1), (7, 1))
F32 = jnp.float32
BF16 = jnp.bfloat16


class Sems:
    sizes = dict(
        group_y=1,
        group_z=1,
        loss_y=1,
        loss_z=1,
        token_y=1,
        stats=1,
        hid_y=RING,
        hid_x=RING,
        hid_relay=RING,
        hid_core=1,
        w_core=1,
        lg_core=1,
        lg_own=len(PIECES),
        lg_relay=len(PIECES),
        x_half=2,
        x_side=1,
        z_half=len(PIECES) * 2,
        z_side=len(PIECES),
    )
    sends = 6

    def __init__(self, recv):
        self.recv, self.base, at = recv, {}, 0
        for name, size in self.sizes.items():
            self.base[name] = at
            at += size

    @classmethod
    def total(cls):
        return sum(cls.sizes.values())

    def of(self, name, index):
        return self.recv.at[self.base[name] + index]


def contract_last(a, b):
    return lax.dot_general(a, b, (((1,), (1,)), ((), ())), preferred_element_type=F32)


def kernel(
    h_hbm, w_hbm, tok_hbm, old_hbm, rew_ref, len_ref, gid_ref, scale_ref,
    loss_ref, gh_ref, gw_ref,
    tok_ref, old_ref, hv, wv, hq, wp, prob, lgg, lgo, lgx, lgp, ht, asend, tok_col, top_col, coef_col, mul_col, stat_col,
    token_rows, y_cols, stat_send, stat_recv, group_y, group_z, loss_y, loss_z,
    x_acc, x_opp, x_side, x_half_in, x_side_in,
    z_acc, z_opp, z_side, z_half_in, z_side_in, gh_buf, gw_buf,
    load_sem, out_sem, send_sem, recv_sem,
):
    tokens, width = hv.shape
    vocab = wv.shape[1]
    half_cols = width // RING // CORES
    z_rows = width // (RING * RING)
    dp, tensor = lax.axis_index("dp"), lax.axis_index("tensor")
    y, z = dp // RING, dp % RING
    x, core = tensor // CORES, tensor % CORES
    sems = Sems(recv_sem)
    sent = [0] * Sems.sends

    def at_y(k):
        return ((y + k) % RING * RING + z, tensor)

    def at_z(k):
        return (y * RING + (z + k) % RING, tensor)

    def at_x(k):
        return (dp, (x + k) % RING * CORES + core)

    def at_tensor(k):
        return (dp, (tensor + k) % (RING * CORES))

    partner = (dp, x * CORES + 1 - core)

    def size_of(ref):
        return math.prod(ref.shape) * ref.dtype.itemsize

    def wait_for(sem, size):
        ref = tok_col if size <= size_of(tok_col) else wv
        row = size_of(ref) // ref.shape[0]
        assert size % (8 * row) == 0, size
        rows = ref.at[pl.ds(0, size // row)]
        pltpu.make_async_copy(rows, rows, sem).wait()

    def put(src, dst, name, index, device):
        if size_of(src) < 2**14:
            slot = 0
        elif name.startswith("z"):
            slot = 1
        else:
            slot = min(range(2, Sems.sends), key=lambda i: sent[i])
        sent[slot] += size_of(src)
        pltpu.make_async_remote_copy(
            src_ref=src,
            dst_ref=dst,
            send_sem=send_sem.at[slot],
            recv_sem=sems.of(name, index),
            device_id=device,
            device_id_type=MESH,
        ).start()

    def arrived(ref, name, index=0, count=1):
        wait_for(sems.of(name, index), size_of(ref) * count)

    k_size = 1024
    k_count = width // k_size
    quarter = [
        pltpu.make_async_copy(
            h_hbm.at[
                pl.ds(pl.multiple_of(x * LANES, LANES), LANES),
                pl.ds(pl.multiple_of(((y + k) % RING * CORES + core) * half_cols, LANES), half_cols),
            ],
            hq.at[k - 1],
            load_sem.at[0],
        )
        for k in range(1, RING)
    ]
    small = [
        pltpu.make_async_copy(tok_hbm, tok_ref, load_sem.at[1]),
        pltpu.make_async_copy(old_hbm, old_ref, load_sem.at[1]),
    ]
    for copy in small + quarter:
        copy.start()

    def load_pair(k):
        return (
            pltpu.make_async_copy(
                h_hbm.at[:, pl.ds(pl.multiple_of(k * k_size, k_size), k_size)],
                hv.at[:, pl.ds(pl.multiple_of(k * k_size, k_size), k_size)],
                load_sem.at[2 + k],
            ),
            pltpu.make_async_copy(
                w_hbm.at[pl.ds(pl.multiple_of(k * k_size, k_size), k_size), :],
                wv.at[pl.ds(pl.multiple_of(k * k_size, k_size), k_size), :],
                load_sem.at[2 + k],
            ),
        )

    for k in range(k_count):
        for copy in load_pair(k):
            copy.start()

    barrier = pltpu.get_barrier_semaphore()
    peers = (
        [at_y(k) for k in range(1, RING)]
        + [at_z(k) for k in range(1, RING)]
        + [at_tensor(k) for k in range(1, RING * CORES)]
    )
    for device in peers:
        pl.semaphore_signal(barrier, inc=1, device_id=device, device_id_type=MESH)

    rolls = rew_ref.shape[0]
    roll_tokens = tokens // rolls
    lane8 = lax.broadcasted_iota(jnp.int32, (8, LANES), 1)
    row8 = lax.broadcasted_iota(jnp.int32, (8, LANES), 0)
    local = jnp.zeros((8, LANES), F32)
    for i in range(rolls):
        value = jnp.where(row8 == 0, rew_ref[i].astype(F32), len_ref[i].astype(F32))
        local += jnp.where((lane8 == gid_ref[i]) & (row8 < 2), value, 0.0)
    group_y[y] = local

    wait_for(load_sem.at[1], size_of(tok_ref) * 2)
    tok = (tok_ref[...] - tensor * vocab).astype(F32)
    for r in range(tokens // LANES):
        tok_col[r * LANES : (r + 1) * LANES, :] = jnp.broadcast_to(tok[r : r + 1, :], (LANES, LANES)).T

    half = pl.ds(pl.multiple_of(core * half_cols, 16), half_cols)
    wait_for(load_sem.at[0], size_of(hq))
    for k in range(1, RING):
        for b in range(half_cols // LANES):
            asend[k - 1, b * LANES : (b + 1) * LANES, :] = hq[k - 1, :, b * LANES : (b + 1) * LANES].T

    def logits(k):
        wait_for(load_sem.at[2 + k], (tokens + vocab) * k_size * 2)

        @pl.loop(0, vocab // 512)
        def _(n):
            cols = pl.ds(pl.multiple_of(n * 512, 512), 512)
            term = jnp.dot(
                hv[:, k * k_size : (k + 1) * k_size],
                wv[k * k_size : (k + 1) * k_size, cols],
                preferred_element_type=F32,
            )
            if k == 0:
                prob[:, cols] = term
            else:
                prob[:, cols] += term

    def send_weights(q):
        rows = pl.ds(pl.multiple_of((q * CORES + 1 - core) * half_cols, 16), half_cols)
        put(w_hbm.at[rows, :], wp.at[q], "w_core", 0, partner)

    logits(0)
    pl.semaphore_wait(barrier, len(peers))
    for k in range(1, RING):
        put(group_y.at[y], group_y.at[y], "group_y", 0, at_y(k))
    for k in (1, 3, 2):
        put(asend.at[k - 1], ht.at[y, x, half, :], "hid_y", k, at_y(k))
    for q in range(RING):
        send_weights(q)
    for k in range(1, k_count):
        logits(k)
        if k == 3:
            arrived(group_y.at[0], "group_y", count=RING - 1)
            group_z[z] = group_y[0] + group_y[1] + group_y[2] + group_y[3]
            for j in range(1, RING):
                put(group_z.at[z], group_z.at[z], "group_z", 0, at_z(j))

    def share_over_x(j):
        block = ht.at[(y + j) % RING, x, half, :]
        arrived(block, "hid_y", RING - j)
        put(block, block, "hid_x", j, at_x(3))
        put(block, block, "hid_x", j, at_x(1))

    front = pl.ds(pl.multiple_of(core * half_cols, 16), half_cols // 2)
    back = pl.ds(pl.multiple_of(core * half_cols + half_cols // 2, 16), half_cols // 2)

    def relay_over_x(j):
        source = (y + j) % RING
        arrived(ht.at[source, x, half, :], "hid_x", j, 2)
        left_block = ht.at[source, (x + 3) % RING, front, :]
        right_block = ht.at[source, (x + 1) % RING, back, :]
        put(left_block, left_block, "hid_relay", j, at_x(1))
        put(right_block, right_block, "hid_relay", j, at_x(3))

    def hand_to_partner(j):
        source = (y + j) % RING
        if j:
            arrived(ht.at[source, x, half, :], "hid_relay", j)
        block = ht.at[source, :, half, :]
        put(block, block, "hid_core", 0, partner)

    step = 32
    lane_step = lax.broadcasted_iota(jnp.int32, (step, LANES), 1)
    lane_step_f = lane_step.astype(F32)
    pieces = vocab // LANES

    @pl.loop(0, tokens // step, unroll=4)
    def _(i):
        rows = pl.ds(pl.multiple_of(i * step, step), step)
        top = prob[rows, 0:LANES]
        for p in range(1, pieces):
            top = jnp.maximum(top, prob[rows, p * LANES : (p + 1) * LANES])
        top_col[rows, :] = jnp.broadcast_to(jnp.max(top, axis=1, keepdims=True), (step, LANES))

    @pl.loop(0, tokens // step, unroll=4)
    def _(i):
        rows = pl.ds(pl.multiple_of(i * step, step), step)
        top, wanted = top_col[rows, :], tok_col[rows, :]
        total = picked = jnp.zeros((step, LANES), F32)
        for p in range(pieces):
            block = prob[rows, p * LANES : (p + 1) * LANES]
            shifted = jnp.exp(block - top)
            prob[rows, p * LANES : (p + 1) * LANES] = shifted
            lgg[y, p, rows, :] = shifted.astype(BF16)
            total += shifted
            picked += jnp.where(lane_step_f + float(p * LANES) == wanted, block, 0.0)
        total = jnp.sum(total, axis=1, keepdims=True)
        picked = jnp.sum(picked, axis=1, keepdims=True)
        stat_col[rows, :] = jnp.where(lane_step == 0, top, jnp.where(lane_step == 1, total, picked))

    def piece(ref, n):
        first, count = PIECES[n]
        return ref.at[pl.ds(first, count)]

    def send_chunk(n):
        block = piece(lgg.at[y], n)
        put(block, block, "lg_own", n, at_y(3))
        put(block, block, "lg_own", n, at_y(1))

    low, high = pl.ds(0, tokens // 2), pl.ds(tokens // 2, tokens // 2)

    def relay_chunk(n):
        from_right, from_left = piece(lgg.at[(y + 1) % RING], n), piece(lgg.at[(y + 3) % RING], n)
        arrived(from_right, "lg_own", n, 2)
        put(from_left.at[:, low], from_left.at[:, low], "lg_relay", n, at_y(1))
        put(from_right.at[:, high], from_right.at[:, high], "lg_relay", n, at_y(3))

    for n in range(2):
        send_chunk(n)

    for r in range(tokens // LANES):
        flipped = stat_col[r * LANES : (r + 1) * LANES, :].T
        for s in range(3):
            stat_send[s * 4 + r : s * 4 + r + 1, :] = flipped[s : s + 1, :]
    stat_send[12:16, :] = jnp.zeros((4, LANES), F32)
    stat_recv[tensor] = stat_send[...]
    for k in range(1, RING * CORES):
        put(stat_send, stat_recv.at[tensor], "stats", 0, at_tensor(k))

    for j in (1, 3):
        share_over_x(j)

    for b in range(half_cols // LANES):
        cols = pl.ds(pl.multiple_of((y * CORES + core) * half_cols + b * LANES, LANES), LANES)
        rows = pl.ds(pl.multiple_of(core * half_cols + b * LANES, LANES), LANES)
        for q in range(RING):
            ht[y, q, rows, :] = hv[q * LANES : (q + 1) * LANES, cols].T

    arrived(group_z.at[0], "group_z", count=RING - 1)
    groups = group_z[0] + group_z[1] + group_z[2] + group_z[3]
    group_wins, group_tokens = groups[0:1, :], groups[1:2, :]
    group_alive = ((group_wins > 0.5) & (group_wins < GROUP - 0.5)).astype(F32)
    token_count = jnp.sum(group_alive * group_tokens, axis=1, keepdims=True)
    divisor = jnp.maximum(token_count, 1.0)
    factor = scale_ref[0] / divisor

    lane4 = lax.broadcasted_iota(jnp.int32, (4, LANES), 1)
    row4 = lax.broadcasted_iota(jnp.int32, (4, LANES), 0)
    token_index = row4 * LANES + lane4
    lane1 = lax.broadcasted_iota(jnp.int32, (1, LANES), 1)
    wins = jnp.zeros((4, LANES), F32)
    reward = jnp.zeros((4, LANES), F32)
    length = jnp.zeros((4, LANES), jnp.int32)
    for i in range(rolls):
        mine = (token_index // roll_tokens) == i
        roll_wins = jnp.sum(jnp.where(lane1 == gid_ref[i], group_wins, 0.0), axis=1, keepdims=True)
        wins = jnp.where(mine, roll_wins, wins)
        reward = jnp.where(mine, rew_ref[i].astype(F32), reward)
        length = jnp.where(mine, len_ref[i], length)
    alive = ((wins > 0.5) & (wins < GROUP - 0.5)).astype(F32)
    spread = jnp.where(alive > 0.5, jnp.sqrt(wins * (GROUP - wins)) / GROUP, 1.0)
    token_adv = alive * (reward - wins / GROUP) / spread
    token_weight = jnp.where(token_index % roll_tokens < length, alive, 0.0)

    arrived(stat_send, "stats", count=RING * CORES - 1)
    share_over_x(2)
    row_top = stat_recv[0, 0:4, :]
    for q in range(1, RING * CORES):
        row_top = jnp.maximum(row_top, stat_recv[q, 0:4, :])
    row_total = jnp.zeros_like(row_top)
    target = jnp.zeros_like(row_top)
    for q in range(RING * CORES):
        row_total += stat_recv[q, 4:8, :] * jnp.exp(stat_recv[q, 0:4, :] - row_top)
        target += stat_recv[q, 8:12, :]
    own_scale = jnp.exp(stat_send[0:4, :] - row_top)

    log_prob = target - row_top - jnp.log(row_total)
    ratio = jnp.exp(log_prob - old_ref[...])
    clipped = jnp.clip(ratio, 1.0 - CLIP_LOW, 1.0 + CLIP_HIGH)
    token_loss = -jnp.minimum(ratio * token_adv, clipped * token_adv)
    active = ratio * token_adv <= clipped * token_adv
    coefficient = jnp.where(active, -token_adv * ratio, 0.0) * token_weight * factor
    multiplier = coefficient * own_scale / row_total
    weighted = jnp.sum(token_weight * token_loss, axis=1, keepdims=True)
    local_loss = weighted[0:1] + weighted[1:2] + weighted[2:3] + weighted[3:4]

    for r in range(tokens // LANES):
        rows = slice(r * LANES, (r + 1) * LANES)
        coef_col[rows, :] = jnp.broadcast_to(coefficient[r : r + 1, :], (LANES, LANES)).T
        mul_col[rows, :] = jnp.broadcast_to(multiplier[r : r + 1, :], (LANES, LANES)).T

    token_rows[y, 0:4, :] = coefficient
    token_rows[y, 4:8, :] = multiplier
    token_rows[y, 8:12, :] = tok
    token_rows[y, 12:16, :] = jnp.zeros((4, LANES), F32)
    for k in (2, 1, 3):
        put(token_rows.at[y], token_rows.at[y], "token_y", 0, at_y(k))

    lane_lg = lax.broadcasted_iota(jnp.int32, (64, LANES), 1).astype(F32)
    for n, (first, count) in enumerate(PIECES):

        @pl.loop(0, tokens // 64)
        def _(i):
            rows = pl.ds(pl.multiple_of(i * 64, 64), 64)
            wanted, coef, mul = tok_col[rows, :], coef_col[rows, :], mul_col[rows, :]
            for p in range(first, first + count):
                hit = jnp.where(lane_lg + float(p * LANES) == wanted, coef, 0.0)
                lgo[p, rows, :] = (hit - prob[rows, p * LANES : (p + 1) * LANES] * mul).astype(BF16)

        put(piece(lgo, n), piece(lgp, n), "lg_core", 0, partner)

    def token_columns():
        arrived(token_rows.at[0], "token_y", count=RING - 1)
        for k in range(1, RING):
            other = (y + k) % RING
            for r in range(tokens // LANES):
                rows = slice(r * LANES, (r + 1) * LANES)
                for i in range(3):
                    line = token_rows[other, i * 4 + r : i * 4 + r + 1, :]
                    y_cols[k - 1, i, rows, :] = jnp.broadcast_to(line, (LANES, LANES)).T

    def gather_gradients(n):
        first, count = PIECES[n]
        for k in range(1, RING):
            other = (y + k) % RING

            @pl.loop(0, tokens // 64)
            def _(i, k=k, other=other):
                rows = pl.ds(pl.multiple_of(i * 64, 64), 64)
                coef, mul, wanted = y_cols[k - 1, 0, rows, :], y_cols[k - 1, 1, rows, :], y_cols[k - 1, 2, rows, :]
                for p in range(count):
                    hit = jnp.where(lane_lg + float((first + p) * LANES) == wanted, coef, 0.0)
                    lgx[k - 1, p, rows, :] = (hit - lgg[other, first + p, rows, :].astype(F32) * mul).astype(BF16)

    loss_y[y] = jnp.broadcast_to(local_loss, (8, LANES))
    for k in range(1, RING):
        put(loss_y.at[y], loss_y.at[y], "loss_y", 0, at_y(k))

    def weight_rows(offset):
        return pl.ds(pl.multiple_of(((x + offset) % RING * CORES + core) * half_cols, 16), half_cols)

    def pair(ref, p):
        return jnp.concatenate([ref[p], ref[p + 1]], axis=1)

    def hidden_block(offset):
        q, rows = (x + offset) % RING, weight_rows(offset)
        result = None
        for p in range(0, pieces, 2):
            cols = slice(p * LANES, (p + 2) * LANES)
            for term in (contract_last(pair(lgo, p), wv[rows, cols]), contract_last(pair(lgp, p), wp[q, :, cols])):
                result = term if result is None else result + term
        return result

    def hidden_blocks(first, last):
        @pl.loop(first, last)
        def _(j):
            x_acc[j] = hidden_block(j + 2)

    hand_to_partner(0)
    arrived(lgp, "lg_core")
    arrived(wp, "w_core")
    hidden_blocks(0, 2)
    x_opp[...] = x_acc[0].astype(BF16)
    mid = tokens // 2
    relay_over_x(1)
    relay_over_x(3)
    relay_chunk(0)
    send_chunk(2)
    hidden_blocks(2, 4)
    relay_over_x(2)
    put(x_opp.at[pl.ds(0, mid)], x_half_in.at[0], "x_half", 0, at_x(3))
    put(x_opp.at[pl.ds(mid, mid)], x_half_in.at[1], "x_half", 1, at_x(1))
    token_columns()
    relay_chunk(1)
    send_chunk(3)
    for j in (1, 3, 2):
        hand_to_partner(j)
    arrived(ht.at[:, :, half, :], "hid_core")

    low_rows = z_rows // 2

    def weight_block(n, offset):
        first, count = PIECES[n]
        rows = pl.ds(pl.multiple_of((z + offset) % RING * z_rows, 16), z_rows)
        result = None
        for k in range(RING):
            s = (y + k) % RING
            for b in range(RING // 2):
                left = jnp.concatenate([ht[s, 2 * b, rows, :], ht[s, 2 * b + 1, rows, :]], axis=1)
                part = slice(b * 256, (b + 1) * 256)
                right = [lgx[k - 1, p, part, :] if k else lgo[first + p, part, :] for p in range(count)]
                right = right[0] if count == 1 else jnp.concatenate(right, axis=1)
                term = jnp.dot(left, right, preferred_element_type=F32)
                result = term if result is None else result + term
        return result

    def columns(n):
        first, count = PIECES[n]
        return pl.ds(first * LANES, count * LANES)

    def weight_chunk(n):
        from_opposite = piece(lgg.at[(y + 2) % RING], n)
        arrived(from_opposite, "lg_relay", n)
        first, count = PIECES[n]
        gather_gradients(n)
        block = weight_block(n, 2).astype(BF16)
        for p in range(count):
            z_opp[first + p] = block[:, p * LANES : (p + 1) * LANES]
        out = piece(z_opp, n)
        put(out.at[:, pl.ds(0, low_rows)], piece(z_half_in.at[0], n), "z_half", 2 * n, at_z(3))
        put(out.at[:, pl.ds(low_rows, low_rows)], piece(z_half_in.at[1], n), "z_half", 2 * n + 1, at_z(1))

        @pl.loop(0, 3)
        def _(j):
            z_acc[j, :, columns(n)] = weight_block(n, j + 3)

    def pass_sides(n):
        first, count = PIECES[n]
        for side, (j, device) in enumerate(((0, at_z(3)), (2, at_z(1)))):
            arrived(piece(z_half_in.at[side], n), "z_half", 2 * n + side)
            summed = slice(side * low_rows, (side + 1) * low_rows)
            plain = slice((1 - side) * low_rows, (2 - side) * low_rows)
            for p in range(first, first + count):
                cols = slice(p * LANES, (p + 1) * LANES)
                z_side[side, p, summed, :] = (z_acc[j, summed, cols] + z_half_in[side, p].astype(F32)).astype(BF16)
                z_side[side, p, plain, :] = z_acc[j, plain, cols].astype(BF16)
            put(piece(z_side.at[side], n), piece(z_side_in.at[side], n), "z_side", n, device)

    def finish_chunk(n):
        first, count = PIECES[n]
        arrived(piece(z_side_in.at[0], n), "z_side", n, 2)
        for p in range(first, first + count):
            cols = slice(p * LANES, (p + 1) * LANES)
            gw_buf[:, cols] = z_acc[1, :, cols] + z_side_in[0, p].astype(F32) + z_side_in[1, p].astype(F32)
        cols = columns(n)
        copy = pltpu.make_async_copy(gw_buf.at[:, cols], gw_ref.at[:, cols], out_sem.at[0])
        copy.start()

    def pass_x_sides():
        arrived(x_half_in.at[0], "x_half", 0)
        x_side[0, 0:mid, :] = (x_acc[1, 0:mid, :] + x_half_in[0].astype(F32)).astype(BF16)
        x_side[0, mid:, :] = x_acc[1, mid:, :].astype(BF16)
        put(x_side.at[0], x_side_in.at[0], "x_side", 0, at_x(3))
        arrived(x_half_in.at[1], "x_half", 1)
        x_side[1, 0:mid, :] = x_acc[3, 0:mid, :].astype(BF16)
        x_side[1, mid:, :] = (x_acc[3, mid:, :] + x_half_in[1].astype(F32)).astype(BF16)
        put(x_side.at[1], x_side_in.at[1], "x_side", 0, at_x(1))

    def finish_x():
        arrived(x_side_in.at[0], "x_side", 0, 2)
        gh_buf[...] = x_acc[2] + x_side_in[0].astype(F32) + x_side_in[1].astype(F32)
        copy = pltpu.make_async_copy(gh_buf, gh_ref, out_sem.at[0])
        copy.start()

    weight_chunk(0)
    arrived(loss_y.at[0], "loss_y", count=RING - 1)
    loss_z[z] = loss_y[0] + loss_y[1] + loss_y[2] + loss_y[3]
    for k in range(1, RING):
        put(loss_z.at[z], loss_z.at[z], "loss_z", 0, at_z(k))
    relay_chunk(2)
    send_chunk(4)
    weight_chunk(1)
    pass_sides(0)
    pass_x_sides()
    relay_chunk(3)
    weight_chunk(2)
    pass_sides(1)
    relay_chunk(4)
    arrived(loss_z.at[0], "loss_z", count=RING - 1)
    loss_total = loss_z[0] + loss_z[1] + loss_z[2] + loss_z[3]
    weight_chunk(3)
    weight_chunk(4)
    pass_sides(2)
    pass_sides(3)
    pass_sides(4)
    finish_chunk(0)
    finish_chunk(1)
    finish_x()
    finish_chunk(2)
    finish_chunk(3)
    finish_chunk(4)
    loss_ref[...] = loss_total[0:1, 0:1] / divisor
    for slot in range(Sems.sends):
        wait_for(send_sem.at[slot], sent[slot])
    wait_for(out_sem.at[0], size_of(gh_buf) + size_of(gw_buf))


def shards(hidden, head_weight, token_ids, old_logprob, rewards, lengths, group_ids, loss_scale):
    tokens, width = hidden.shape
    vocab = head_weight.shape[1]
    pieces = vocab // LANES
    half_cols = width // RING // CORES
    z_rows = width // (RING * RING)
    rows = tokens // LANES
    hbm = pl.BlockSpec(memory_space=pl.ANY)
    vmem = pl.BlockSpec(memory_space=pltpu.VMEM)
    smem = pl.BlockSpec(memory_space=pltpu.SMEM)
    loss, grad_hidden, grad_weight = pl.pallas_call(
        kernel,
        out_shape=(
            jax.ShapeDtypeStruct((1, 1), F32),
            jax.ShapeDtypeStruct((tokens, half_cols), F32),
            jax.ShapeDtypeStruct((z_rows, vocab), F32),
        ),
        in_specs=[hbm, hbm, hbm, hbm, smem, smem, smem, smem],
        out_specs=(vmem, hbm, hbm),
        scratch_shapes=[
            pltpu.VMEM((rows, LANES), jnp.int32),
            pltpu.VMEM((rows, LANES), F32),
            pltpu.VMEM((tokens, width), BF16),
            pltpu.VMEM((width, vocab), BF16),
            pltpu.VMEM((RING - 1, LANES, half_cols), BF16),
            pltpu.VMEM((RING, half_cols, vocab), BF16),
            pltpu.VMEM((tokens, vocab), F32),
            pltpu.VMEM((RING, pieces, tokens, LANES), BF16),
            pltpu.VMEM((pieces, tokens, LANES), BF16),
            pltpu.VMEM((RING - 1, 2, tokens, LANES), BF16),
            pltpu.VMEM((pieces, tokens, LANES), BF16),
            pltpu.VMEM((RING, RING, half_cols * CORES, LANES), BF16),
            pltpu.VMEM((RING - 1, half_cols, LANES), BF16),
            pltpu.VMEM((tokens, LANES), F32),
            pltpu.VMEM((tokens, LANES), F32),
            pltpu.VMEM((tokens, LANES), F32),
            pltpu.VMEM((tokens, LANES), F32),
            pltpu.VMEM((tokens, LANES), F32),
            pltpu.VMEM((RING, 16, LANES), F32),
            pltpu.VMEM((RING - 1, 3, tokens, LANES), F32),
            pltpu.VMEM((16, LANES), F32),
            pltpu.VMEM((RING * CORES, 16, LANES), F32),
            pltpu.VMEM((RING, 8, LANES), F32),
            pltpu.VMEM((RING, 8, LANES), F32),
            pltpu.VMEM((RING, 8, LANES), F32),
            pltpu.VMEM((RING, 8, LANES), F32),
            pltpu.VMEM((RING, tokens, half_cols), F32),
            pltpu.VMEM((tokens, half_cols), BF16),
            pltpu.VMEM((2, tokens, half_cols), BF16),
            pltpu.VMEM((2, tokens // 2, half_cols), BF16),
            pltpu.VMEM((2, tokens, half_cols), BF16),
            pltpu.VMEM((3, z_rows, vocab), F32),
            pltpu.VMEM((pieces, z_rows, LANES), BF16),
            pltpu.VMEM((2, pieces, z_rows, LANES), BF16),
            pltpu.VMEM((2, pieces, z_rows // 2, LANES), BF16),
            pltpu.VMEM((2, pieces, z_rows, LANES), BF16),
            pltpu.VMEM((tokens, half_cols), F32),
            pltpu.VMEM((z_rows, vocab), F32),
            pltpu.SemaphoreType.DMA((2 + width // 1024,)),
            pltpu.SemaphoreType.DMA((1,)),
            pltpu.SemaphoreType.DMA((Sems.sends,)),
            pltpu.SemaphoreType.DMA((Sems.total(),)),
        ],
        compiler_params=pltpu.CompilerParams(
            collective_id=0, has_side_effects=True, vmem_limit_bytes=66_000_000
        ),
        name="policy_step",
    )(
        hidden,
        head_weight,
        token_ids.reshape(rows, LANES),
        old_logprob.reshape(rows, LANES),
        rewards,
        lengths,
        group_ids,
        loss_scale.reshape(1),
    )
    return (loss.reshape(()), grad_hidden, grad_weight)


def solution(mesh):
    return jax.shard_map(
        shards,
        mesh=mesh,
        in_specs=(
            P("dp", None),
            P(None, "tensor"),
            P("dp"),
            P("dp"),
            P("dp"),
            P("dp"),
            P("dp"),
            P(),
        ),
        out_specs=(P(), P("dp", "tensor"), P("dp", "tensor")),
        check_vma=False,
    )
```

time: 89.6 us -> 73.3 us (0.82)
  Pallas kernels: 82.8 us -> 66.5 us
    pallas_call x1, Pallas kernels: 82.8 us -> 66.5 us  [shards(): pl.pallas_call(kernel, out_shape=(jax.ShapeDtypeStruct((1, 1), F32), jax....]
where the time goes in v2:
time: 73.3 us; the launch traced here: 73.1 us
  Pallas kernels  66.5 us (91%)
  local copies, waits for them, and re-layouts  3.62 us (5%)
  between operations  2.98 us (4%)
    pallas_call x1, Pallas kernels, shards(): pl.pallas_call(kernel, out_shape=(jax.ShapeDtypeStruct((1, 1), F32), jax....  66.5 us
    unnamed x4, local copies, waits for them, and re-layouts  3.62 us

profile of v2, /device:TPU:0, one launch (start us, length us, event | category | flops | bytes accessed | tf_op | source)
XLA Modules:
  0.0 73.1 jit_solution(4273392611944914490)
XLA Ops:
  1.3 66.5 %policy_step.1 = (f32[1,1]{1,0:T(1,128)}, f32[512,640]{1,0:T(8,128)}, f32[320,1024]{1,0:T(8,128)}) custom-call(bf16[512,5120]{1,0:T(8,128)(2,1)} %h_hbm.1, bf16[5120,1024]{1,0:T(8,128)(2,1)} %w_hbm.1, s32[4,128]{1,0:T(4,128)} %bitcast.5, f32[4,128]{1,0:T(4,128)} %bitcast.6, s32[8]{0:T(128)} %rew_ref.1, s32[8]{0:T(128)} %len_ref.1, s32[8]{0:T(128)} %gid_ref.1, ...), custom_call_target="tpu_custom_call" | custom-call | tf_op jit(solution)/shard_map/policy_step/pallas_call | solution.py:580
  68.4 0.0 copy-start
  68.4 2.6 %copy.16 = f32[512,640]{1,0:T(8,128)} copy(f32[512,640]{1,0:T(8,128)} %get-tuple-element.13) | data formatting | bytes 2621440
  70.9 0.0 copy-done
  70.9 1.1 %copy.17 = f32[320,1024]{1,0:T(8,128)} copy(f32[320,1024]{1,0:T(8,128)S(1)} %copy-done) | data formatting | bytes 2621440
Async XLA Ops:
  68.4 2.6 %copy-start = (f32[320,1024]{1,0:T(8,128)S(1)}, f32[320,1024]{1,0:T(8,128)}, u32[]{:S(2)}) copy-start(f32[320,1024]{1,0:T(8,128)} %get-tuple-element.14) | copy-start | bytes 3932164
